TPU v7x, 32 devices: a 4x4x1 block of a 4x4x8 slice. The times are simulated.
32 devices in a mesh: dp: 1 (over z), tp: 32 (over y, x, core).
Axes of the slice: x: 4, y: 4, z: 1, core: 2. Of those that a mesh axis runs over, the one named last changes fastest.
The devices are a block of a 4x4x8 slice.
Arguments:
- x_norm: bfloat16 [256, 5120], P(('dp', 'tp'))
- w_gate: bfloat16 [5120, 13824], P(None, 'tp')
- w_up: bfloat16 [5120, 13824], P(None, 'tp')
- w_down: bfloat16 [13824, 5120], P('tp')
- u_gate: bfloat16 [256, 13824], P('dp', 'tp')
- u_up: bfloat16 [256, 13824], P('dp', 'tp')
- grad_out: bfloat16 [256, 5120], P(('dp', 'tp'))
Outputs:
- output 1: bfloat16 [256, 5120], P(('dp', 'tp'))
- output 2: float32 [5120, 13824], P('dp', 'tp')
- output 3: float32 [5120, 13824], P('dp', 'tp')
- output 4: float32 [13824, 5120], P(('dp', 'tp'))
All inputs are finite; a program needn't handle non-finite values.
Results may differ from a plain program's by a relative error of at most 0.0134744.
Values are sent between devices in bfloat16 or wider.
A program may use at most 768 MiB of HBM per device.

v0:
```python
import functools
import math

import jax
import jax.numpy as jnp
from jax import lax
from jax.experimental import pallas as pl
from jax.experimental.pallas import tpu as pltpu
from jax.sharding import PartitionSpec as P

MESH = pl.DeviceIdType.MESH
BF16 = jnp.bfloat16
F32 = jnp.float32
CORES = 2
COL_TILE = 512
SLOTS = 4
MXU_TILE = 256
MERGED = 1
GROUPS = (2, 2, 1)
VMEM_BYTES = 67043328
NT = (((1,), (1,)), ((), ()))


def comm_kernel(ring, n_copies, x_hbm, dy_hbm, wd_hbm, wg_hbm, wu_hbm, ug_hbm, uu_hbm,
                dx_ref, xf, dyf, dg_t, du_t, z_t,
                wd, wg, wu, ug, uu, gate, up, mid, dgs, dus, pb, pr, sx, sy,
                lf, mg, rw, rm, lf2, mg2, rw2, rm2, lsem, ssem, rsem):
    R = ring
    me = lax.axis_index("tp")
    c = lax.rem(me, CORES)
    x = lax.rem(me // CORES, R)
    y = me // (CORES * R)
    oc = 1 - c
    rows, hidden = x_hbm.shape
    tokens = R * R * CORES * rows
    H2, Q = hidden // 2, hidden // 4
    xs = [lax.rem(x + d, R) for d in range(R)]
    ys = [lax.rem(y + d, R) for d in range(R)]

    def dev(yy, xx, cc):
        return {"tp": (yy * R + xx) * CORES + cc}

    def at(axis, s, core):
        return dev(y, xs[s % R], core) if axis == 0 else dev(ys[s % R], x, core)

    steps = [(axis, s) for axis in (0, 1) for s in (1, -1, 2)]
    nbr = {step: at(*step, c) for step in steps}
    across = {step: at(*step, oc) for step in steps}
    to_core = [{step: at(*step, core) for step in steps} for core in range(CORES)]
    mate = dev(y, x, oc)

    def local(src, dst, i):
        cp = pltpu.make_async_copy(src, dst, lsem.at[i])
        cp.start()
        return cp

    cp_dy = local(dy_hbm, dyf.at[y, x, c], 0)
    cp_x = local(x_hbm, xf.at[y, x, c], 1)
    cp_ug = local(ug_hbm, ug, 2)
    cp_uu = local(uu_hbm, uu, 3)
    cp_wd = local(wd_hbm, wd, 4)
    cp_wg = local(wg_hbm, wg, 5)
    cp_wu = local(wu_hbm, wu, 6)

    barrier = pltpu.get_barrier_semaphore()
    for d in (*nbr.values(), *across.values(), mate):
        pl.semaphore_signal(barrier, inc=1, device_id=d, device_id_type=MESH)
    pl.semaphore_wait(barrier, 2 * len(nbr) + 1)

    sent = []

    class Copy:
        def __init__(self, make, device):
            self.make, self.device, self.i = make, device, len(sent)
            sent.append(self)
            self.describe().start()

        def describe(self):
            src, dst = self.make()
            return pltpu.make_async_remote_copy(src_ref=src, dst_ref=dst, send_sem=ssem.at[self.i],
                                                recv_sem=rsem.at[self.i], device_id=self.device,
                                                device_id_type=MESH)

        def wait_recv(self):
            self.describe().wait_recv()

        def wait_send(self):
            self.describe().wait_send()

    def send(src, dst, device):
        return Copy(lambda: (src, dst), device)

    def share(make, device):
        return Copy(lambda: (make(), make()), device)

    class Half:
        def __init__(self, buf, first, own):
            self.buf, self.first, self.own = buf, first, own
            base = first * H2
            self.all, self.lo, self.hi = pl.ds(base, H2), pl.ds(base, Q), pl.ds(base + Q, Q)
            self.near, self.far, self.rows = {}, {}, {}

        def ref(self, d1, d2, cols, cores=slice(None)):
            if self.first == 0:
                return self.buf.at[ys[d2], xs[d1], cores, :, cols]
            return self.buf.at[ys[d1], xs[d2], cores, :, cols]

        def push(self, key, d1, axis, core=None):
            cores = slice(None) if core is None else pl.ds(core, 1)
            ref = functools.partial(self.ref, d1, 0, self.all, cores)
            to = to_core[self.own]
            self.near.setdefault(key, []).append((share(ref, to[axis, 1]), share(ref, to[axis, -1])))
            return ref

        def relay(self, key, minus, plus, axis):
            for cp, _ in self.near[key]:
                cp.wait_recv()
            a = share(functools.partial(self.ref, *minus, self.lo), nbr[axis, 1])
            for _, cp in self.near[key]:
                cp.wait_recv()
            self.far[key] = [a, share(functools.partial(self.ref, *plus, self.hi), nbr[axis, -1])]

        def first_send(self, core):
            self.push("f", 0, self.first, core)

        def first_direct(self, core):
            ref = self.push("f", 0, self.first, core)
            self.far.setdefault("f", []).append(share(ref, to_core[self.own][self.first, 2]))

        def first_near(self):
            for pair in self.near["f"]:
                for cp in pair:
                    cp.wait_recv()

        def first_relay(self):
            self.relay("f", (R - 1, 0), (1, 0), self.first)

        def first_far(self):
            for cp in self.far["f"]:
                cp.wait_recv()

        def second_home(self, core):
            self.push(0, 0, 1 - self.first, core)

        def second_send(self, d1):
            self.push(d1, d1, 1 - self.first)

        def second_relay(self, d1):
            self.relay(d1, (d1, R - 1), (d1, 1), 1 - self.first)

        def second_far(self, d1):
            for cp in self.far[d1]:
                cp.wait_recv()

        def to_mate(self, d2):
            def ref():
                if self.first == 0:
                    return self.buf.at[ys[d2], :, :, :, self.all]
                return self.buf.at[:, xs[d2], :, :, self.all]

            self.rows[d2] = share(ref, mate)

        def spot_to_mate(self, d1, d2, cores=slice(None)):
            self.rows[d1, d2] = share(functools.partial(self.ref, d1, d2, self.all, cores), mate)

        def home_to_mate(self):
            self.spot_to_mate(0, 0, pl.ds(self.own, 1))
            for d1 in range(1, R):
                self.spot_to_mate(d1, 0)

        def mate_rows(self, row):
            for key, cp in self.rows.items():
                if key == row or (isinstance(key, tuple) and key[1] == row):
                    cp.wait_recv()

    class Gather:
        def __init__(self, buf, own):
            self.halves = (Half(buf, 0, own), Half(buf, 1, own))

        def __getattr__(self, name):
            def both(*args):
                for h in self.halves:
                    getattr(h, name)(*args)
            return both

    def prepare():
        g_f = ug[...].astype(F32)
        u_f = uu[...].astype(F32)
        z_t[...] = (g_f * jax.nn.sigmoid(g_f) * u_f).astype(BF16)
        gate[...] = g_f.T
        up[...] = u_f.T

    def grads():
        mid[...] = lax.dot_general(dyf[...].reshape(tokens, hidden), wd[...], NT, preferred_element_type=F32)
        step = tokens // 8
        for i in range(8):
            tok = pl.ds(i * step, step)
            g_mid, g_f, u_f = mid[tok, :], gate[tok, :], up[tok, :]
            s = jax.nn.sigmoid(g_f)
            dgs[tok, :] = (g_mid * u_f * s * (1.0 + g_f * (1.0 - s))).astype(BF16)
            dus[tok, :] = (g_mid * (g_f * s)).astype(BF16)

    kinds = ((0, 1, 0), (1, 1, H2), (0, -1, Q), (1, -1, H2 + Q))
    widths = [t * MXU_TILE for t in GROUPS]
    starts = [sum(widths[:g]) for g in range(len(widths))]
    pair, leaf, raw, merged, leaf2, raw2, merged2 = {}, {}, {}, {}, {}, {}, {}

    def piece_cols(n, g):
        return pl.ds(kinds[n][2] + starts[g], widths[g])

    def partial(n, g):
        dg, du = dgs[...], dus[...]
        for t in range(GROUPS[g]):
            cols = pl.ds(kinds[n][2] + starts[g] + t * MXU_TILE, MXU_TILE)
            p = (jnp.dot(dg, wg[:, cols], preferred_element_type=F32)
                 + jnp.dot(du, wu[:, cols], preferred_element_type=F32))
            pb[:, :, :, :, cols] = p.astype(BF16).reshape(R, R, CORES, rows, MXU_TILE)
        cols = piece_cols(n, g)
        pair[n, g] = send(pb.at[:, :, oc, :, cols], pr.at[:, :, :, cols], mate)

    def line(n, d, cols):
        if kinds[n][0] == 0:
            return sx.at[:, xs[d], :, cols]
        return sx.at[ys[d], :, :, cols]

    def spot(n, d):
        return (ys if kinds[n][0] == 0 else xs)[d]

    def scatter_first(n, g):
        axis, s, _ = kinds[n]
        cols = piece_cols(n, g)
        pair[n, g].wait_recv()
        for yy in range(R):
            sx[yy, :, :, cols] = pb[yy, :, c, :, cols].astype(F32) + pr[yy, :, :, cols].astype(F32)
        leaf[n, g] = send(line(n, 2, cols), lf.at[:, :, cols], nbr[axis, s])

    def scatter_raw(n, g):
        axis, s, _ = kinds[n]
        cols = piece_cols(n, g)
        raw[n, g] = send(line(n, -s % R, cols), rw.at[:, :, cols], nbr[axis, -s])

    def scatter_merge(n, g):
        axis, s, _ = kinds[n]
        cols = piece_cols(n, g)
        leaf[n, g].wait_recv()
        mg[:, :, cols] = lf[:, :, cols] + line(n, s % R, cols)[...]
        merged[n, g] = send(mg.at[:, :, cols], rm.at[:, :, cols], nbr[axis, s])

    def scatter_second(n, g):
        axis, s, _ = kinds[n]
        cols = piece_cols(n, g)
        raw[n, g].wait_recv()
        merged[n, g].wait_recv()
        sy[:, :, cols] = line(n, 0, cols)[...] + rm[:, :, cols] + rw[:, :, cols]
        direct = g >= MERGED
        leaf2[n, g] = send(sy.at[spot(n, 2), :, cols], lf2.at[:, cols], nbr[1 - axis, 2 if direct else s])
        if direct:
            merged2[n, g] = send(sy.at[spot(n, s % R), :, cols], rm2.at[:, cols], nbr[1 - axis, s])
        raw2[n, g] = send(sy.at[spot(n, -s % R), :, cols], rw2.at[:, cols], nbr[1 - axis, -s])

    def scatter_merge2(n, g):
        assert g < MERGED
        axis, s, _ = kinds[n]
        cols = piece_cols(n, g)
        leaf2[n, g].wait_recv()
        mg2[:, cols] = lf2[:, cols] + sy[spot(n, s % R), :, cols]
        merged2[n, g] = send(mg2.at[:, cols], rm2.at[:, cols], nbr[1 - axis, s])

    def scatter_last(n, g):
        cols = piece_cols(n, g)
        raw2[n, g].wait_recv()
        merged2[n, g].wait_recv()
        total = sy[spot(n, 0), :, cols] + rm2[:, cols] + rw2[:, cols]
        if g >= MERGED:
            leaf2[n, g].wait_recv()
            total = total + lf2[:, cols]
        dx_ref[:, cols] = total.astype(BF16)

    def pieces(f, g):
        for n in range(len(kinds)):
            f(n, g)

    def transposes():
        dg_t[...] = dgs[...].astype(F32).T.astype(BF16)
        du_t[...] = dus[...].astype(F32).T.astype(BF16)

    gd, gx = Gather(dyf, 1), Gather(xf, 0)
    only = ([], [])

    def on(core):
        def run(f):
            @pl.when(c == core)
            def _():
                n = len(sent)
                f()
                only[core].extend(sent[n:])
        return run

    cp_dy.wait()
    swap = []

    @on(0)
    def _():
        gd.first_direct(0)
        gd.second_home(0)
        swap.append(share(lambda: dyf.at[y, x, 0], mate))
        cp_x.wait()
        gx.first_send(0)
        cp_ug.wait()
        cp_uu.wait()
        prepare()

    @on(1)
    def _():
        gd.first_direct(1)
        gd.second_home(1)
        cp_x.wait()
        gx.first_send(1)
        swap.append(share(lambda: xf.at[y, x, 1], mate))
        cp_ug.wait()
        cp_uu.wait()
        prepare()
        gd.first_near()
        gd.second_send(R - 1)
        gd.second_send(1)
        gd.first_far()
        gd.second_send(2)
        gd.second_relay(0)
        swap[0].wait_recv()
        gd.home_to_mate()
        gd.second_relay(R - 1)
        gd.second_relay(1)
        gd.second_relay(2)
        gd.to_mate(R - 1)
        gd.to_mate(1)
        gx.second_home(1)
        gd.second_far(0)
        gd.spot_to_mate(0, 2)
        gd.second_far(R - 1)
        gd.spot_to_mate(R - 1, 2)
        gd.second_far(1)
        gd.spot_to_mate(1, 2)
        gd.second_far(2)
        gd.spot_to_mate(2, 2)
        cp_wd.wait()

    @on(0)
    def _():
        gx.first_relay()
        gd.mate_rows(0)
        gx.first_far()
        gd.mate_rows(R - 1)
        gd.mate_rows(1)
        gx.second_home(0)
        gx.second_send(R - 1)
        gx.second_send(1)
        gx.second_send(2)
        cp_wd.wait()
        gd.mate_rows(2)

    grads()

    @on(0)
    def _():
        gx.second_relay(0)

    cp_wg.wait()
    cp_wu.wait()
    partial(0, 0)
    partial(1, 0)
    partial(2, 0)

    @on(0)
    def _():
        gx.second_relay(R - 1)

    partial(3, 0)
    scatter_first(0, 0)
    scatter_first(1, 0)
    partial(0, 1)
    scatter_first(2, 0)
    scatter_first(3, 0)

    @on(0)
    def _():
        gx.second_relay(1)

    pieces(scatter_raw, 0)
    partial(1, 1)
    partial(2, 1)

    @on(0)
    def _():
        gx.second_relay(2)

    partial(3, 1)
    partial(0, 2)
    scatter_first(0, 1)
    scatter_first(1, 1)
    partial(1, 2)
    scatter_first(2, 1)
    scatter_first(3, 1)
    pieces(scatter_merge, 0)
    partial(2, 2)
    partial(3, 2)
    pieces(scatter_raw, 1)
    pieces(scatter_first, 2)

    @on(0)
    def _():
        swap[1].wait_recv()
        gx.home_to_mate()
        gx.to_mate(R - 1)
        gx.to_mate(1)

    pieces(scatter_merge, 1)
    pieces(scatter_raw, 2)
    transposes()
    pieces(scatter_second, 0)
    pieces(scatter_merge, 2)
    pieces(scatter_merge2, 0)
    pieces(scatter_second, 1)

    @on(0)
    def _():
        gx.second_far(0)
        gx.second_far(R - 1)
        gx.second_far(1)
        gx.second_far(2)
        gx.to_mate(2)

    pieces(scatter_second, 2)

    @on(1)
    def _():
        for d in range(R):
            gx.mate_rows(d)

    pieces(scatter_last, 0)
    pieces(scatter_last, 1)
    pieces(scatter_last, 2)
    common = [cp for cp in sent if not any(cp is other for other in only[0] + only[1])]
    for core in range(CORES):
        @on(core)
        def _():
            for cp in list(only[core]):
                cp.wait_send()

    for cp in common:
        cp.wait_send()
    assert len(sent) == n_copies, len(sent)


def weight_kernel(xf, dyf, dg_t, du_t, z_t, dx, og, ou, od, odx, buf, sem, dx_sem):
    slots, tile = buf.shape[1], buf.shape[3]
    tokens, hidden = dg_t.shape[1], og.shape[1]
    out = pltpu.make_async_copy(dx, odx, dx_sem)
    out.start()
    jobs = ((dg_t, xf, og), (du_t, xf, ou), (z_t, dyf, od))
    flight = {}
    for t in range(hidden // tile):
        cols = pl.ds(t * tile, tile)
        for i, (lhs, rhs, dst) in enumerate(jobs):
            slot = t % slots
            if (i, t - slots) in flight:
                flight[i, t - slots].wait()
            buf[i, slot] = jnp.dot(lhs[...], rhs[:, :, :, :, cols].reshape(tokens, tile), preferred_element_type=F32)
            flight[i, t] = pltpu.make_async_copy(buf.at[i, slot], dst.at[:, cols], sem.at[i, slot])
            flight[i, t].start()
    for t in range(hidden // tile - slots, hidden // tile):
        for i in range(len(jobs)):
            flight[i, t].wait()
    out.wait()


def solution(mesh):
    tp = mesh.shape["tp"]
    ring = math.isqrt(tp // CORES)

    def local_backward(x_loc, wg_loc, wu_loc, wd_loc, ug_loc, uu_loc, dy_loc):
        rows, hidden = x_loc.shape
        ffn = wd_loc.shape[0]
        tokens = tp * rows
        R = ring
        n_copies = 2 + 2 * (6 + 4 * R + 3 * R) + 2 * (8 + 4 * R + 2 * R - 1) + 4 * len(GROUPS) * 7
        full = (R, R, CORES, rows, hidden)
        vm = pltpu.VMEM
        out_bytes = 2 * (rows * hidden + 2 * tokens * hidden + 3 * ffn * tokens)
        dx, xf, dyf, dg_t, du_t, z_t = pl.pallas_call(
            lambda *refs: comm_kernel(R, n_copies, *refs),
            name="comm",
            out_shape=(vm((rows, hidden), BF16), vm(full, BF16), vm(full, BF16),
                       vm((ffn, tokens), BF16), vm((ffn, tokens), BF16), vm((ffn, tokens), BF16)),
            in_specs=[pl.BlockSpec(memory_space=pltpu.HBM)] * 7,
            out_specs=(pl.BlockSpec(memory_space=vm),) * 6,
            scratch_shapes=[
                vm((ffn, hidden), BF16), vm((ffn, hidden), BF16), vm((ffn, hidden), BF16),
                vm((ffn, tokens), BF16), vm((ffn, tokens), BF16),
                vm((tokens, ffn), F32), vm((tokens, ffn), F32), vm((tokens, ffn), F32),
                vm((tokens, ffn), BF16), vm((tokens, ffn), BF16),
                vm(full, BF16), vm((R, R, rows, hidden), BF16),
                vm((R, R, rows, hidden), F32), vm((R, rows, hidden), F32),
                *[vm((R, rows, hidden), F32)] * 4, *[vm((rows, hidden), F32)] * 4,
                pltpu.SemaphoreType.DMA((7,)),
                pltpu.SemaphoreType.DMA((n_copies,)),
                pltpu.SemaphoreType.DMA((n_copies,)),
            ],
            compiler_params=pltpu.CompilerParams(collective_id=0, has_side_effects=True,
                                                 vmem_limit_bytes=VMEM_BYTES - out_bytes - 40960),
        )(x_loc, dy_loc, wd_loc, wg_loc.T, wu_loc.T, ug_loc.T, uu_loc.T)
        out = jax.ShapeDtypeStruct((ffn, hidden), F32)
        hbm = pl.BlockSpec(memory_space=pltpu.HBM)
        gw_g, gw_u, gw_d, dx = pl.pallas_call(
            weight_kernel,
            name="weight_grads",
            out_shape=(out, out, out, jax.ShapeDtypeStruct((rows, hidden), BF16)),
            in_specs=[pl.BlockSpec(memory_space=vm)] * 6,
            out_specs=(hbm,) * 4,
            scratch_shapes=[vm((3, SLOTS, ffn, COL_TILE), F32), pltpu.SemaphoreType.DMA((3, SLOTS)),
                            pltpu.SemaphoreType.DMA],
            compiler_params=pltpu.CompilerParams(vmem_limit_bytes=24 << 20),
        )(xf, dyf, dg_t, du_t, z_t, dx)
        return dx, gw_g.T, gw_u.T, gw_d

    row_spec = P(("dp", "tp"), None)
    col_spec = P(None, "tp")
    part_cols = P("dp", "tp")
    return jax.shard_map(local_backward, mesh=mesh,
                         in_specs=(row_spec, col_spec, col_spec, P("tp", None), part_cols, part_cols, row_spec),
                         out_specs=(row_spec, part_cols, part_cols, row_spec),
                         check_vma=False)
```

profile of v0, /device:TPU:96, one launch (start us, length us, event | category | flops | bytes accessed | tf_op | source)
XLA Modules:
  0.0 58.0 jit_solution(2039566793747270333)
XLA Ops:
  0.6 48.0 %comm.1 = (bf16[8,5120]{1,0:T(8,128)(2,1)S(1)}, bf16[4,4,2,8,5120]{4,3,2,1,0:T(8,128)(2,1)S(1)}, bf16[4,4,2,8,5120]{4,3,2,1,0:T(8,128)(2,1)S(1)}, bf16[432,256]{...) custom-call(bf16[8,5120]{1,0:T(8,128)(2,1)} %refs_0_.1, bf16[8,5120]{1,0:T(8,128)(2,1)} %refs_1_.1, ...), custom_call_target="tpu_custom_call" | custom-call | tf_op jit(solution)/shard_map/comm/pallas_call | solution.py:489
  48.6 9.2 %weight_grads.1 = (f32[432,5120]{1,0:T(8,128)}, f32[432,5120]{1,0:T(8,128)}, f32[432,5120]{1,0:T(8,128)}, bf16[8,5120]{1,0:T(8,128)(2,1)}) custom-call(bf16[4,4,2,8,5120]{4,3,2,1,0:T(8,128)(2,1)S(1)} %get-tuple-element.14.xf, bf16[4,4,2,8,5120]{4,3,2,1,0:T(8,128)(2,1)S(1)} %get-tuple-element.15.dyf, bf16[432,256]{1,0:T(8,128)(2,1)S(1)} %get-tuple-element.16.dg_t, ...), custom_call_target="tpu_custom_call" | custom-call | tf_op jit(solution)/shard_map/weight_grads/pallas_call | solution.py:513
where the time goes:
time: 58 us
  Pallas kernels  57.1 us (98%)
  between operations  0.8 us (1%)
    pallas_call x1, Pallas kernels, local_backward(): pl.pallas_call(lambda *refs: comm_kernel(R, n_copies, *refs), name='comm'...  48 us
    pallas_call x1, Pallas kernels, local_backward(): pl.pallas_call(weight_kernel, name='weight_grads', out_shape=(out, out, o...  9.17 us

commit v1 on v0

--- a/solution.py
+++ b/solution.py
@@ -12,11 +12,11 @@
 BF16 = jnp.bfloat16
 F32 = jnp.float32
 CORES = 2
-COL_TILE = 512
-SLOTS = 4
+COL_TILE = 1024
+SLOTS = 3
 MXU_TILE = 256
-MERGED = 1
-GROUPS = (2, 2, 1)
+MERGED = 0
+GROUPS = (1, 2, 1, 1)
 VMEM_BYTES = 67043328
 NT = (((1,), (1,)), ((), ()))
 
@@ -349,50 +349,40 @@
         gx.first_relay()
         gd.mate_rows(0)
         gx.first_far()
-        gd.mate_rows(R - 1)
-        gd.mate_rows(1)
         gx.second_home(0)
         gx.second_send(R - 1)
         gx.second_send(1)
         gx.second_send(2)
+        gd.mate_rows(R - 1)
+        gd.mate_rows(1)
+        gx.second_relay(0)
         cp_wd.wait()
         gd.mate_rows(2)
 
     grads()
 
-    @on(0)
-    def _():
-        gx.second_relay(0)
-
+    def x_relay(d1):
+        @on(0)
+        def _():
+            gx.second_relay(d1)
+
+    x_relay(R - 1)
     cp_wg.wait()
     cp_wu.wait()
     partial(0, 0)
     partial(1, 0)
     partial(2, 0)
-
-    @on(0)
-    def _():
-        gx.second_relay(R - 1)
-
     partial(3, 0)
+    x_relay(1)
+    partial(0, 1)
     scatter_first(0, 0)
     scatter_first(1, 0)
-    partial(0, 1)
+    partial(1, 1)
     scatter_first(2, 0)
     scatter_first(3, 0)
-
-    @on(0)
-    def _():
-        gx.second_relay(1)
-
     pieces(scatter_raw, 0)
-    partial(1, 1)
+    x_relay(2)
     partial(2, 1)
-
-    @on(0)
-    def _():
-        gx.second_relay(2)
-
     partial(3, 1)
     partial(0, 2)
     scatter_first(0, 1)
@@ -401,10 +391,20 @@
     scatter_first(2, 1)
     scatter_first(3, 1)
     pieces(scatter_merge, 0)
+    pieces(scatter_raw, 1)
     partial(2, 2)
     partial(3, 2)
-    pieces(scatter_raw, 1)
-    pieces(scatter_first, 2)
+    partial(0, 3)
+    scatter_first(0, 2)
+    scatter_first(1, 2)
+    partial(1, 3)
+    scatter_first(2, 2)
+    scatter_first(3, 2)
+    partial(2, 3)
+    partial(3, 3)
+    pieces(scatter_raw, 2)
+    pieces(scatter_merge, 1)
+    pieces(scatter_first, 3)
 
     @on(0)
     def _():
@@ -413,12 +413,11 @@
         gx.to_mate(R - 1)
         gx.to_mate(1)
 
-    pieces(scatter_merge, 1)
-    pieces(scatter_raw, 2)
+    pieces(scatter_raw, 3)
+    pieces(scatter_merge, 2)
     transposes()
     pieces(scatter_second, 0)
-    pieces(scatter_merge, 2)
-    pieces(scatter_merge2, 0)
+    pieces(scatter_merge, 3)
     pieces(scatter_second, 1)
 
     @on(0)
@@ -430,15 +429,15 @@
         gx.to_mate(2)
 
     pieces(scatter_second, 2)
+    pieces(scatter_second, 3)
 
     @on(1)
     def _():
         for d in range(R):
             gx.mate_rows(d)
 
-    pieces(scatter_last, 0)
-    pieces(scatter_last, 1)
-    pieces(scatter_last, 2)
+    for g in range(len(GROUPS)):
+        pieces(scatter_last, g)
     common = [cp for cp in sent if not any(cp is other for other in only[0] + only[1])]
     for core in range(CORES):
         @on(core)
@@ -518,7 +517,7 @@
             out_specs=(hbm,) * 4,
             scratch_shapes=[vm((3, SLOTS, ffn, COL_TILE), F32), pltpu.SemaphoreType.DMA((3, SLOTS)),
                             pltpu.SemaphoreType.DMA],
-            compiler_params=pltpu.CompilerParams(vmem_limit_bytes=24 << 20),
+            compiler_params=pltpu.CompilerParams(vmem_limit_bytes=28 << 20),
         )(xf, dyf, dg_t, du_t, z_t, dx)
         return dx, gw_g.T, gw_u.T, gw_d
 

time: 58 us -> 59.3 us (1.022)
  Pallas kernels: 57.1 us -> 58.4 us
    pallas_call x1, Pallas kernels: 48 us -> 49.1 us  [local_backward(): pl.pallas_call(lambda *refs: comm_kernel(R, n_copies, *refs), name='comm'...]
where the time goes in v1:
time: 59.3 us; the launch traced here: 59.2 us
  Pallas kernels  58.4 us (98%)
  between operations  0.8 us (1%)
    pallas_call x1, Pallas kernels, local_backward(): pl.pallas_call(lambda *refs: comm_kernel(R, n_copies, *refs), name='comm'...  49.1 us
    pallas_call x1, Pallas kernels, local_backward(): pl.pallas_call(weight_kernel, name='weight_grads', out_shape=(out, out, o...  9.29 us

profile of v1, /device:TPU:96, one launch (start us, length us, event | category | flops | bytes accessed | tf_op | source)
XLA Modules:
  0.0 59.2 jit_solution(13336645811172463439)
XLA Ops:
  0.6 49.1 %comm.1 = (bf16[8,5120]{1,0:T(8,128)(2,1)S(1)}, bf16[4,4,2,8,5120]{4,3,2,1,0:T(8,128)(2,1)S(1)}, bf16[4,4,2,8,5120]{4,3,2,1,0:T(8,128)(2,1)S(1)}, bf16[432,256]{...) custom-call(bf16[8,5120]{1,0:T(8,128)(2,1)} %refs_0_.1, bf16[8,5120]{1,0:T(8,128)(2,1)} %refs_1_.1, ...), custom_call_target="tpu_custom_call" | custom-call | tf_op jit(solution)/shard_map/comm/pallas_call | solution.py:488
  49.8 9.3 %weight_grads.1 = (f32[432,5120]{1,0:T(8,128)}, f32[432,5120]{1,0:T(8,128)}, f32[432,5120]{1,0:T(8,128)}, bf16[8,5120]{1,0:T(8,128)(2,1)}) custom-call(bf16[4,4,2,8,5120]{4,3,2,1,0:T(8,128)(2,1)S(1)} %get-tuple-element.14.xf, bf16[4,4,2,8,5120]{4,3,2,1,0:T(8,128)(2,1)S(1)} %get-tuple-element.15.dyf, bf16[432,256]{1,0:T(8,128)(2,1)S(1)} %get-tuple-element.16.dg_t, ...), custom_call_target="tpu_custom_call" | custom-call | tf_op jit(solution)/shard_map/weight_grads/pallas_call | solution.py:512

commit v2 on v0

--- a/solution.py
+++ b/solution.py
@@ -12,8 +12,8 @@
 BF16 = jnp.bfloat16
 F32 = jnp.float32
 CORES = 2
-COL_TILE = 512
-SLOTS = 4
+COL_TILE = 256
+SLOTS = 8
 MXU_TILE = 256
 MERGED = 1
 GROUPS = (2, 2, 1)
@@ -208,15 +208,17 @@
     def piece_cols(n, g):
         return pl.ds(kinds[n][2] + starts[g], widths[g])
 
-    def partial(n, g):
+    def partial(g, *ns):
         dg, du = dgs[...], dus[...]
-        for t in range(GROUPS[g]):
-            cols = pl.ds(kinds[n][2] + starts[g] + t * MXU_TILE, MXU_TILE)
-            p = (jnp.dot(dg, wg[:, cols], preferred_element_type=F32)
-                 + jnp.dot(du, wu[:, cols], preferred_element_type=F32))
-            pb[:, :, :, :, cols] = p.astype(BF16).reshape(R, R, CORES, rows, MXU_TILE)
-        cols = piece_cols(n, g)
-        pair[n, g] = send(pb.at[:, :, oc, :, cols], pr.at[:, :, :, cols], mate)
+        for n in ns:
+            for t in range(GROUPS[g]):
+                cols = pl.ds(kinds[n][2] + starts[g] + t * MXU_TILE, MXU_TILE)
+                p = (jnp.dot(dg, wg[:, cols], preferred_element_type=F32)
+                     + jnp.dot(du, wu[:, cols], preferred_element_type=F32))
+                pb[:, :, :, :, cols] = p.astype(BF16).reshape(R, R, CORES, rows, MXU_TILE)
+        for n in ns:
+            cols = piece_cols(n, g)
+            pair[n, g] = send(pb.at[:, :, oc, :, cols], pr.at[:, :, :, cols], mate)
 
     def line(n, d, cols):
         if kinds[n][0] == 0:
@@ -349,60 +351,48 @@
         gx.first_relay()
         gd.mate_rows(0)
         gx.first_far()
-        gd.mate_rows(R - 1)
-        gd.mate_rows(1)
         gx.second_home(0)
         gx.second_send(R - 1)
         gx.second_send(1)
         gx.second_send(2)
+        gd.mate_rows(R - 1)
+        gd.mate_rows(1)
+        gx.second_relay(0)
         cp_wd.wait()
         gd.mate_rows(2)
 
     grads()
 
-    @on(0)
-    def _():
-        gx.second_relay(0)
+    def x_relay(d1):
+        @on(0)
+        def _():
+            gx.second_relay(d1)
 
     cp_wg.wait()
     cp_wu.wait()
     partial(0, 0)
-    partial(1, 0)
-    partial(2, 0)
-
-    @on(0)
-    def _():
-        gx.second_relay(R - 1)
-
-    partial(3, 0)
+    partial(0, 1)
+    partial(0, 2)
+    partial(0, 3)
     scatter_first(0, 0)
     scatter_first(1, 0)
-    partial(0, 1)
+    x_relay(R - 1)
+    partial(1, 0)
     scatter_first(2, 0)
     scatter_first(3, 0)
-
-    @on(0)
-    def _():
-        gx.second_relay(1)
-
+    x_relay(1)
     pieces(scatter_raw, 0)
     partial(1, 1)
-    partial(2, 1)
-
-    @on(0)
-    def _():
-        gx.second_relay(2)
-
-    partial(3, 1)
-    partial(0, 2)
+    x_relay(2)
+    partial(1, 2)
+    partial(1, 3)
+    partial(2, 0, 1)
     scatter_first(0, 1)
     scatter_first(1, 1)
-    partial(1, 2)
+    partial(2, 2, 3)
     scatter_first(2, 1)
     scatter_first(3, 1)
     pieces(scatter_merge, 0)
-    partial(2, 2)
-    partial(3, 2)
     pieces(scatter_raw, 1)
     pieces(scatter_first, 2)
 
@@ -418,8 +408,8 @@
     transposes()
     pieces(scatter_second, 0)
     pieces(scatter_merge, 2)
+    pieces(scatter_second, 1)
     pieces(scatter_merge2, 0)
-    pieces(scatter_second, 1)
 
     @on(0)
     def _():
@@ -518,7 +508,7 @@
             out_specs=(hbm,) * 4,
             scratch_shapes=[vm((3, SLOTS, ffn, COL_TILE), F32), pltpu.SemaphoreType.DMA((3, SLOTS)),
                             pltpu.SemaphoreType.DMA],
-            compiler_params=pltpu.CompilerParams(vmem_limit_bytes=24 << 20),
+            compiler_params=pltpu.CompilerParams(vmem_limit_bytes=28 << 20),
         )(xf, dyf, dg_t, du_t, z_t, dx)
         return dx, gw_g.T, gw_u.T, gw_d
 

time: 58 us -> 61.6 us (1.062)
  Pallas kernels: 57.1 us -> 60.7 us
    pallas_call x1, Pallas kernels: 9.17 us -> 12.5 us  [local_backward(): pl.pallas_call(weight_kernel, name='weight_grads', out_shape=(out, out, o...]
where the time goes in v2:
time: 61.6 us; the launch traced here: 61.5 us
  Pallas kernels  60.7 us (99%)
  between operations  0.8 us (1%)
    pallas_call x1, Pallas kernels, local_backward(): pl.pallas_call(lambda *refs: comm_kernel(R, n_copies, *refs), name='comm'...  48.3 us
    pallas_call x1, Pallas kernels, local_backward(): pl.pallas_call(weight_kernel, name='weight_grads', out_shape=(out, out, o...  12.5 us

profile of v2, /device:TPU:96, one launch (start us, length us, event | category | flops | bytes accessed | tf_op | source)
XLA Modules:
  0.0 61.5 jit_solution(1186905436104703120)
XLA Ops:
  0.6 48.3 %comm.1 = (bf16[8,5120]{1,0:T(8,128)(2,1)S(1)}, bf16[4,4,2,8,5120]{4,3,2,1,0:T(8,128)(2,1)S(1)}, bf16[4,4,2,8,5120]{4,3,2,1,0:T(8,128)(2,1)S(1)}, bf16[432,256]{...) custom-call(bf16[8,5120]{1,0:T(8,128)(2,1)} %refs_0_.1, bf16[8,5120]{1,0:T(8,128)(2,1)} %refs_1_.1, ...), custom_call_target="tpu_custom_call" | custom-call | tf_op jit(solution)/shard_map/comm/pallas_call | solution.py:479
  48.9 12.5 %weight_grads.1 = (f32[432,5120]{1,0:T(8,128)}, f32[432,5120]{1,0:T(8,128)}, f32[432,5120]{1,0:T(8,128)}, bf16[8,5120]{1,0:T(8,128)(2,1)}) custom-call(bf16[4,4,2,8,5120]{4,3,2,1,0:T(8,128)(2,1)S(1)} %get-tuple-element.14.xf, bf16[4,4,2,8,5120]{4,3,2,1,0:T(8,128)(2,1)S(1)} %get-tuple-element.15.dyf, bf16[432,256]{1,0:T(8,128)(2,1)S(1)} %get-tuple-element.16.dg_t, ...), custom_call_target="tpu_custom_call" | custom-call | tf_op jit(solution)/shard_map/weight_grads/pallas_call | solution.py:503

commit v3 on v2

--- a/solution.py
+++ b/solution.py
@@ -12,8 +12,8 @@
 BF16 = jnp.bfloat16
 F32 = jnp.float32
 CORES = 2
-COL_TILE = 256
-SLOTS = 8
+COL_TILE = 512
+SLOTS = 4
 MXU_TILE = 256
 MERGED = 1
 GROUPS = (2, 2, 1)
@@ -71,7 +71,7 @@
 
     class Copy:
         def __init__(self, make, device):
-            self.make, self.device, self.i = make, device, len(sent)
+            self.make, self.device, self.i, self.left = make, device, len(sent), False
             sent.append(self)
             self.describe().start()
 
@@ -85,7 +85,9 @@
             self.describe().wait_recv()
 
         def wait_send(self):
-            self.describe().wait_send()
+            if not self.left:
+                self.describe().wait_send()
+            self.left = True
 
     def send(src, dst, device):
         return Copy(lambda: (src, dst), device)
@@ -110,7 +112,6 @@
             ref = functools.partial(self.ref, d1, 0, self.all, cores)
             to = to_core[self.own]
             self.near.setdefault(key, []).append((share(ref, to[axis, 1]), share(ref, to[axis, -1])))
-            return ref
 
         def relay(self, key, minus, plus, axis):
             for cp, _ in self.near[key]:
@@ -124,7 +125,7 @@
             self.push("f", 0, self.first, core)
 
         def first_direct(self, core):
-            ref = self.push("f", 0, self.first, core)
+            ref = functools.partial(self.ref, 0, 0, self.all, pl.ds(core, 1))
             self.far.setdefault("f", []).append(share(ref, to_core[self.own][self.first, 2]))
 
         def first_near(self):
@@ -303,21 +304,25 @@
 
     @on(0)
     def _():
+        gd.first_send(0)
+        gd.second_home(0)
         gd.first_direct(0)
-        gd.second_home(0)
+        gate = sent[-2:]
         swap.append(share(lambda: dyf.at[y, x, 0], mate))
         cp_x.wait()
-        gx.first_send(0)
         cp_ug.wait()
         cp_uu.wait()
         prepare()
+        for cp in gate:
+            cp.wait_send()
+        gx.first_send(0)
 
     @on(1)
     def _():
+        gd.first_send(1)
+        gd.second_home(1)
         gd.first_direct(1)
-        gd.second_home(1)
         cp_x.wait()
-        gx.first_send(1)
         swap.append(share(lambda: xf.at[y, x, 1], mate))
         cp_ug.wait()
         cp_uu.wait()
@@ -325,6 +330,7 @@
         gd.first_near()
         gd.second_send(R - 1)
         gd.second_send(1)
+        gx.first_send(1)
         gd.first_far()
         gd.second_send(2)
         gd.second_relay(0)

time: 61.6 us -> 60.6 us (0.984)
  Pallas kernels: 60.7 us -> 59.7 us
    pallas_call x1, Pallas kernels: 12.5 us -> 9.17 us  [local_backward(): pl.pallas_call(weight_kernel, name='weight_grads', out_shape=(out, out, o...]
    pallas_call x1, Pallas kernels: 48.3 us -> 50.5 us  [local_backward(): pl.pallas_call(lambda *refs: comm_kernel(R, n_copies, *refs), name='comm'...]
where the time goes in v3:
time: 60.6 us; the launch traced here: 60.5 us
  Pallas kernels  59.7 us (99%)
  between operations  0.8 us (1%)
    pallas_call x1, Pallas kernels, local_backward(): pl.pallas_call(lambda *refs: comm_kernel(R, n_copies, *refs), name='comm'...  50.5 us
    pallas_call x1, Pallas kernels, local_backward(): pl.pallas_call(weight_kernel, name='weight_grads', out_shape=(out, out, o...  9.17 us

profile of v3, /device:TPU:96, one launch (start us, length us, event | category | flops | bytes accessed | tf_op | source)
XLA Modules:
  0.0 60.5 jit_solution(13698964058434522672)
XLA Ops:
  0.6 50.5 %comm.1 = (bf16[8,5120]{1,0:T(8,128)(2,1)S(1)}, bf16[4,4,2,8,5120]{4,3,2,1,0:T(8,128)(2,1)S(1)}, bf16[4,4,2,8,5120]{4,3,2,1,0:T(8,128)(2,1)S(1)}, bf16[432,256]{...) custom-call(bf16[8,5120]{1,0:T(8,128)(2,1)} %refs_0_.1, bf16[8,5120]{1,0:T(8,128)(2,1)} %refs_1_.1, ...), custom_call_target="tpu_custom_call" | custom-call | tf_op jit(solution)/shard_map/comm/pallas_call | solution.py:485
  51.2 9.2 %weight_grads.1 = (f32[432,5120]{1,0:T(8,128)}, f32[432,5120]{1,0:T(8,128)}, f32[432,5120]{1,0:T(8,128)}, bf16[8,5120]{1,0:T(8,128)(2,1)}) custom-call(bf16[4,4,2,8,5120]{4,3,2,1,0:T(8,128)(2,1)S(1)} %get-tuple-element.14.xf, bf16[4,4,2,8,5120]{4,3,2,1,0:T(8,128)(2,1)S(1)} %get-tuple-element.15.dyf, bf16[432,256]{1,0:T(8,128)(2,1)S(1)} %get-tuple-element.16.dg_t, ...), custom_call_target="tpu_custom_call" | custom-call | tf_op jit(solution)/shard_map/weight_grads/pallas_call | solution.py:509

commit v4 on v3

--- a/solution.py
+++ b/solution.py
@@ -307,15 +307,12 @@
         gd.first_send(0)
         gd.second_home(0)
         gd.first_direct(0)
-        gate = sent[-2:]
         swap.append(share(lambda: dyf.at[y, x, 0], mate))
         cp_x.wait()
+        gx.first_send(0)
         cp_ug.wait()
         cp_uu.wait()
         prepare()
-        for cp in gate:
-            cp.wait_send()
-        gx.first_send(0)
 
     @on(1)
     def _():
@@ -323,6 +320,7 @@
         gd.second_home(1)
         gd.first_direct(1)
         cp_x.wait()
+        gx.first_send(1)
         swap.append(share(lambda: xf.at[y, x, 1], mate))
         cp_ug.wait()
         cp_uu.wait()
@@ -330,10 +328,10 @@
         gd.first_near()
         gd.second_send(R - 1)
         gd.second_send(1)
-        gx.first_send(1)
         gd.first_far()
         gd.second_send(2)
         gd.second_relay(0)
+        gx.second_home(1)
         swap[0].wait_recv()
         gd.home_to_mate()
         gd.second_relay(R - 1)
@@ -341,7 +339,6 @@
         gd.second_relay(2)
         gd.to_mate(R - 1)
         gd.to_mate(1)
-        gx.second_home(1)
         gd.second_far(0)
         gd.spot_to_mate(0, 2)
         gd.second_far(R - 1)
@@ -355,9 +352,9 @@
     @on(0)
     def _():
         gx.first_relay()
+        gx.second_home(0)
         gd.mate_rows(0)
         gx.first_far()
-        gx.second_home(0)
         gx.second_send(R - 1)
         gx.second_send(1)
         gx.second_send(2)

time: 60.6 us -> 58.5 us (0.965)
  Pallas kernels: 59.7 us -> 57.7 us
    pallas_call x1, Pallas kernels: 50.5 us -> 48.5 us  [local_backward(): pl.pallas_call(lambda *refs: comm_kernel(R, n_copies, *refs), name='comm'...]
where the time goes in v4:
time: 58.5 us
  Pallas kernels  57.7 us (99%)
  between operations  0.8 us (1%)
    pallas_call x1, Pallas kernels, local_backward(): pl.pallas_call(lambda *refs: comm_kernel(R, n_copies, *refs), name='comm'...  48.5 us
    pallas_call x1, Pallas kernels, local_backward(): pl.pallas_call(weight_kernel, name='weight_grads', out_shape=(out, out, o...  9.17 us

profile of v4, /device:TPU:96, one launch (start us, length us, event | category | flops | bytes accessed | tf_op | source)
XLA Modules:
  0.0 58.5 jit_solution(13236415476648826527)
XLA Ops:
  0.6 48.5 %comm.1 = (bf16[8,5120]{1,0:T(8,128)(2,1)S(1)}, bf16[4,4,2,8,5120]{4,3,2,1,0:T(8,128)(2,1)S(1)}, bf16[4,4,2,8,5120]{4,3,2,1,0:T(8,128)(2,1)S(1)}, bf16[432,256]{...) custom-call(bf16[8,5120]{1,0:T(8,128)(2,1)} %refs_0_.1, bf16[8,5120]{1,0:T(8,128)(2,1)} %refs_1_.1, ...), custom_call_target="tpu_custom_call" | custom-call | tf_op jit(solution)/shard_map/comm/pallas_call | solution.py:482
  49.1 9.2 %weight_grads.1 = (f32[432,5120]{1,0:T(8,128)}, f32[432,5120]{1,0:T(8,128)}, f32[432,5120]{1,0:T(8,128)}, bf16[8,5120]{1,0:T(8,128)(2,1)}) custom-call(bf16[4,4,2,8,5120]{4,3,2,1,0:T(8,128)(2,1)S(1)} %get-tuple-element.14.xf, bf16[4,4,2,8,5120]{4,3,2,1,0:T(8,128)(2,1)S(1)} %get-tuple-element.15.dyf, bf16[432,256]{1,0:T(8,128)(2,1)S(1)} %get-tuple-element.16.dg_t, ...), custom_call_target="tpu_custom_call" | custom-call | tf_op jit(solution)/shard_map/weight_grads/pallas_call | solution.py:506

commit v5 on v2

--- a/solution.py
+++ b/solution.py
@@ -12,8 +12,8 @@
 BF16 = jnp.bfloat16
 F32 = jnp.float32
 CORES = 2
-COL_TILE = 256
-SLOTS = 8
+COL_TILE = 512
+SLOTS = 4
 MXU_TILE = 256
 MERGED = 1
 GROUPS = (2, 2, 1)
@@ -351,13 +351,12 @@
         gx.first_relay()
         gd.mate_rows(0)
         gx.first_far()
+        gd.mate_rows(R - 1)
+        gd.mate_rows(1)
         gx.second_home(0)
         gx.second_send(R - 1)
         gx.second_send(1)
         gx.second_send(2)
-        gd.mate_rows(R - 1)
-        gd.mate_rows(1)
-        gx.second_relay(0)
         cp_wd.wait()
         gd.mate_rows(2)
 
@@ -376,12 +375,13 @@
     partial(0, 3)
     scatter_first(0, 0)
     scatter_first(1, 0)
-    x_relay(R - 1)
+    x_relay(0)
     partial(1, 0)
     scatter_first(2, 0)
     scatter_first(3, 0)
+    x_relay(R - 1)
+    pieces(scatter_raw, 0)
     x_relay(1)
-    pieces(scatter_raw, 0)
     partial(1, 1)
     x_relay(2)
     partial(1, 2)
@@ -508,7 +508,7 @@
             out_specs=(hbm,) * 4,
             scratch_shapes=[vm((3, SLOTS, ffn, COL_TILE), F32), pltpu.SemaphoreType.DMA((3, SLOTS)),
                             pltpu.SemaphoreType.DMA],
-            compiler_params=pltpu.CompilerParams(vmem_limit_bytes=28 << 20),
+            compiler_params=pltpu.CompilerParams(vmem_limit_bytes=24 << 20),
         )(xf, dyf, dg_t, du_t, z_t, dx)
         return dx, gw_g.T, gw_u.T, gw_d
 

time: 61.6 us -> 59 us (0.958)
  Pallas kernels: 60.7 us -> 58.1 us
    pallas_call x1, Pallas kernels: 12.5 us -> 9.17 us  [local_backward(): pl.pallas_call(weight_kernel, name='weight_grads', out_shape=(out, out, o...]
    pallas_call x1, Pallas kernels: 48.3 us -> 48.9 us  [local_backward(): pl.pallas_call(lambda *refs: comm_kernel(R, n_copies, *refs), name='comm'...]
where the time goes in v5:
time: 59 us; the launch traced here: 58.9 us
  Pallas kernels  58.1 us (98%)
  between operations  0.8 us (1%)
    pallas_call x1, Pallas kernels, local_backward(): pl.pallas_call(lambda *refs: comm_kernel(R, n_copies, *refs), name='comm'...  48.9 us
    pallas_call x1, Pallas kernels, local_backward(): pl.pallas_call(weight_kernel, name='weight_grads', out_shape=(out, out, o...  9.17 us

profile of v5, /device:TPU:96, one launch (start us, length us, event | category | flops | bytes accessed | tf_op | source)
XLA Modules:
  0.0 58.9 jit_solution(9696107583682659148)
XLA Ops:
  0.6 48.9 %comm.1 = (bf16[8,5120]{1,0:T(8,128)(2,1)S(1)}, bf16[4,4,2,8,5120]{4,3,2,1,0:T(8,128)(2,1)S(1)}, bf16[4,4,2,8,5120]{4,3,2,1,0:T(8,128)(2,1)S(1)}, bf16[432,256]{...) custom-call(bf16[8,5120]{1,0:T(8,128)(2,1)} %refs_0_.1, bf16[8,5120]{1,0:T(8,128)(2,1)} %refs_1_.1, ...), custom_call_target="tpu_custom_call" | custom-call | tf_op jit(solution)/shard_map/comm/pallas_call | solution.py:479
  49.6 9.2 %weight_grads.1 = (f32[432,5120]{1,0:T(8,128)}, f32[432,5120]{1,0:T(8,128)}, f32[432,5120]{1,0:T(8,128)}, bf16[8,5120]{1,0:T(8,128)(2,1)}) custom-call(bf16[4,4,2,8,5120]{4,3,2,1,0:T(8,128)(2,1)S(1)} %get-tuple-element.14.xf, bf16[4,4,2,8,5120]{4,3,2,1,0:T(8,128)(2,1)S(1)} %get-tuple-element.15.dyf, bf16[432,256]{1,0:T(8,128)(2,1)S(1)} %get-tuple-element.16.dg_t, ...), custom_call_target="tpu_custom_call" | custom-call | tf_op jit(solution)/shard_map/weight_grads/pallas_call | solution.py:503

commit v6 on v5

--- a/solution.py
+++ b/solution.py
@@ -362,37 +362,47 @@
 
     grads()
 
-    def x_relay(d1):
-        @on(0)
-        def _():
-            gx.second_relay(d1)
+    @on(0)
+    def _():
+        gx.second_relay(0)
 
     cp_wg.wait()
     cp_wu.wait()
     partial(0, 0)
     partial(0, 1)
     partial(0, 2)
+
+    @on(0)
+    def _():
+        gx.second_relay(R - 1)
+
     partial(0, 3)
     scatter_first(0, 0)
     scatter_first(1, 0)
-    x_relay(0)
     partial(1, 0)
     scatter_first(2, 0)
     scatter_first(3, 0)
-    x_relay(R - 1)
+
+    @on(0)
+    def _():
+        gx.second_relay(1)
+
     pieces(scatter_raw, 0)
-    x_relay(1)
     partial(1, 1)
-    x_relay(2)
     partial(1, 2)
+
+    @on(0)
+    def _():
+        gx.second_relay(2)
+
     partial(1, 3)
     partial(2, 0, 1)
     scatter_first(0, 1)
     scatter_first(1, 1)
-    partial(2, 2, 3)
     scatter_first(2, 1)
     scatter_first(3, 1)
     pieces(scatter_merge, 0)
+    partial(2, 2, 3)
     pieces(scatter_raw, 1)
     pieces(scatter_first, 2)
 
@@ -408,8 +418,8 @@
     transposes()
     pieces(scatter_second, 0)
     pieces(scatter_merge, 2)
+    pieces(scatter_merge2, 0)
     pieces(scatter_second, 1)
-    pieces(scatter_merge2, 0)
 
     @on(0)
     def _():

time: 59 us -> 58.6 us (level)
  no operation moved by 1% of the time
where the time goes in v6:
time: 58.6 us; the launch traced here: 58.5 us
  Pallas kernels  57.7 us (98%)
  between operations  0.8 us (1%)
    pallas_call x1, Pallas kernels, local_backward(): pl.pallas_call(lambda *refs: comm_kernel(R, n_copies, *refs), name='comm'...  48.6 us
    pallas_call x1, Pallas kernels, local_backward(): pl.pallas_call(weight_kernel, name='weight_grads', out_shape=(out, out, o...  9.17 us

profile of v6, /device:TPU:96, one launch (start us, length us, event | category | flops | bytes accessed | tf_op | source)
XLA Modules:
  0.0 58.5 jit_solution(10700037824541034806)
XLA Ops:
  0.6 48.6 %comm.1 = (bf16[8,5120]{1,0:T(8,128)(2,1)S(1)}, bf16[4,4,2,8,5120]{4,3,2,1,0:T(8,128)(2,1)S(1)}, bf16[4,4,2,8,5120]{4,3,2,1,0:T(8,128)(2,1)S(1)}, bf16[432,256]{...) custom-call(bf16[8,5120]{1,0:T(8,128)(2,1)} %refs_0_.1, bf16[8,5120]{1,0:T(8,128)(2,1)} %refs_1_.1, ...), custom_call_target="tpu_custom_call" | custom-call | tf_op jit(solution)/shard_map/comm/pallas_call | solution.py:489
  49.2 9.2 %weight_grads.1 = (f32[432,5120]{1,0:T(8,128)}, f32[432,5120]{1,0:T(8,128)}, f32[432,5120]{1,0:T(8,128)}, bf16[8,5120]{1,0:T(8,128)(2,1)}) custom-call(bf16[4,4,2,8,5120]{4,3,2,1,0:T(8,128)(2,1)S(1)} %get-tuple-element.14.xf, bf16[4,4,2,8,5120]{4,3,2,1,0:T(8,128)(2,1)S(1)} %get-tuple-element.15.dyf, bf16[432,256]{1,0:T(8,128)(2,1)S(1)} %get-tuple-element.16.dg_t, ...), custom_call_target="tpu_custom_call" | custom-call | tf_op jit(solution)/shard_map/weight_grads/pallas_call | solution.py:513
